TPU v7x, 32 devices: a whole 2x2x4 slice. The times are simulated.
32 devices in a mesh: cuts: 8 (over y, x, core), mode: 4 (over z).
Axes of the slice: x: 2, y: 2, z: 4, core: 2. Of those that a mesh axis runs over, the one named last changes fastest.
Arguments:
- stem: float32 [8, 16, 16, 32768], P('cuts', 'mode'), may hold values from -1.5 to 1.5
- left: float32 [6, 2, 512, 512], P(None, None, 'mode'), may hold values from -0.25 to 0.25
- right: float32 [512, 512], replicated, may hold values from -0.25 to 0.25
- slice_bits: int32 [8, 6], P('cuts'), may hold values from 0 to 1
- leg_order: int32 [6, 9], replicated, may hold values from 0 to 8, each once within a row
Outputs:
- amplitudes: float32 [16, 16, 32768], P(None, 'mode', 'cuts')
Inputs may be any that keep to these rules, and one draw needn't show every extreme that they name: slice_bits[s, t] is the value of branch t's cut bond in slice s. Each row of leg_order is a permutation of 0 to 8.
All inputs are finite; a program needn't handle non-finite values.
Results may differ from a plain program's by a relative error of at most 0.00018.
Values sent between devices are 32-bit elements; how exact they have to be, the bound alone decides.
No kernel may reach another device: no remote copies, remote signals or barrier semaphores. Data moves between devices by JAX's collectives and lax.ppermute only.
A program may use at most 128 MiB of HBM per device.

v0:
```python
import jax
import jax.numpy as jnp
from jax import lax
from jax.sharding import PartitionSpec as P

HIGHEST_PRECISION = lax.Precision.HIGHEST


def leg_columns(leg_map, leg_count):
    indices = jnp.arange(2**leg_count, dtype=jnp.int32)
    shifts = leg_count - 1 - leg_map
    chosen = jnp.right_shift(indices[:, None], shifts[None, :]) & 1
    powers = jnp.left_shift(
        jnp.ones((leg_count,), jnp.int32), leg_count - 1 - jnp.arange(leg_count, dtype=jnp.int32)
    )
    return jnp.sum(chosen * powers[None, :], axis=1)


def per_device(stem, left, right, slice_bits, leg_order):
    slices, leading, middle, trailing = stem.shape
    leg_count = leg_order.shape[1]
    branch_size = 2**leg_count
    total_modes = 8 + trailing.bit_length() - 1
    devices_mode = lax.axis_size("mode")
    picked = jnp.where((slice_bits == 1)[:, :, None, None], left[None, :, 1], left[None, :, 0])

    def branch_right(branch):
        return jnp.take(right, leg_columns(leg_order[branch], leg_count), axis=1)

    def build(fragment, permuted):
        count_a, count_b, width = fragment.shape
        product = jnp.dot(
            fragment.reshape(count_a * count_b, width), permuted, precision=HIGHEST_PRECISION
        )
        return product.reshape(count_a, count_b, branch_size)

    def fetch(branch, kernel):
        return kernel(
            lax.all_gather(
                build(picked[:, branch], branch_right(branch)), "mode", axis=1, tiled=True
            ),
            jnp.int32(0),
        )

    def run_absorb(tensor, first, branch):
        after = 2 ** (total_modes - first - leg_count)
        prefix = tensor.shape[1] // (branch_size * after)
        if after == 1:
            shaped = tensor.reshape(slices, prefix, branch_size)

            def kernel(fragment, offset):
                return jnp.einsum("sji,spi->spj", fragment, shaped, precision=HIGHEST_PRECISION)

        else:
            shaped = tensor.reshape(slices, prefix, branch_size, after)

            def kernel(fragment, offset):
                return jnp.einsum("sji,spir->spjr", fragment, shaped, precision=HIGHEST_PRECISION)

        return fetch(branch, kernel).reshape(slices, -1)

    tensor = stem.reshape(slices, -1)
    tensor = run_absorb(tensor, total_modes - leg_count, 0)
    tensor = run_absorb(tensor, 6, 1)
    tensor = run_absorb(tensor, 4, 2)
    columns = middle // devices_mode
    head_states = leading * devices_mode
    inner_head = 2 ** (leg_count - 4)
    head_matrix = lax.all_gather(build(picked[:, 3], branch_right(3)), "mode", axis=1, tiled=True)
    head_blocks = head_matrix.reshape(slices, head_states, inner_head, head_states, inner_head)
    blocks = tensor.reshape(
        slices, leading, devices_mode, columns, inner_head, trailing // inner_head
    )
    received = lax.all_to_all(blocks, "mode", split_axis=2, concat_axis=1, tiled=True)
    arranged = received.reshape(slices, head_states, columns, inner_head, received.shape[5])
    result = jnp.einsum("sabcd,scxdr->saxbr", head_blocks, arranged, precision=HIGHEST_PRECISION)
    tensor = result.reshape(slices, -1)
    tensor = run_absorb(tensor, total_modes - leg_count, 4)
    inner_pair = 2 ** (leg_count - 2)
    shaped_pair = tensor.reshape(slices, 4, 4, columns, inner_pair, -1)

    def pair_kernel(fragment, offset):
        pieces = fragment.reshape(slices, fragment.shape[1], 4, inner_pair)
        return jnp.einsum("sjce,sacxer->sjaxr", pieces, shaped_pair, precision=HIGHEST_PRECISION)

    result = fetch(5, pair_kernel)
    result = result.reshape(slices, 4, inner_pair, 4, columns, -1).transpose(0, 3, 1, 4, 2, 5)
    tensor = result.reshape(slices, head_states, columns, trailing)
    summed = jnp.sum(tensor, axis=0)
    return lax.psum_scatter(summed, "cuts", scatter_dimension=2, tiled=True)


def solution(mesh):
    in_specs = (
        P("cuts", "mode", None, None),
        P(None, None, "mode", None),
        P(),
        P("cuts", None),
        P(),
    )
    out_specs = P(None, "mode", "cuts")
    return jax.shard_map(
        per_device, mesh=mesh, in_specs=in_specs, out_specs=out_specs, check_vma=False
    )
```

profile of v0, /device:TPU:0, one launch (start us, length us, event | category | flops | bytes accessed | tf_op | source)
XLA Modules:
  0.0 568.9 jit_solution(1955522628350760730)
XLA Ops:
  29.0 9.4 %reshape.121 = f32[4096,512]{1,0:T(8,128)} reshape(f32[1,4,16,32768]{3,2,1,0:T(8,128)} %param.7) | data formatting | bytes 16777216 | tf_op jit(solution)/shard_map/reshape.2
  38.4 10.2 %all-gather.15.cloned.1.call-done = f32[512,512]{1,0:T(8,128)} async-done(((f32[128,512]{1,0:T(8,128)}), f32[512,512]{1,0:T(8,128)}) %all-gather.15.cloned.1.call-update) | async-done | bytes 1048592 | tf_op jit(solution)/shard_map/all_gather | solution.py:39
  48.6 17.5 %convolution_bitcast_fusion = f32[4096,512]{0,1:T(8,128)} fusion(f32[512,512]{1,0:T(8,128)} %all-gather.15.cloned.1.call-done, f32[4096,512]{1,0:T(8,128)} %reshape.121), kind=kOutput, calls=%fused_computation.9 | convolution fusion | flops 12884901888 | bytes 17825792 | tf_op jit(solution)/shard_map/sji,spi->spj/dot_general | solution.py:52
  66.0 9.0 %copy.55 = f32[4096,512]{1,0:T(8,128)} copy(f32[4096,512]{0,1:T(8,128)} %convolution_bitcast_fusion) | data formatting | bytes 16777216 | tf_op jit(solution)/shard_map/sji,spi->spj/dot_general | solution.py:52
  75.0 9.4 %reshape.122 = f32[16,512,256]{2,1,0:T(8,128)} reshape(f32[4096,512]{1,0:T(8,128)} %copy.55) | data formatting | bytes 16777216 | tf_op jit(solution)/shard_map/reshape.6
  84.4 30.5 %convolution_bitcast_fusion.1 = f32[1,16,512,256]{2,3,1,0:T(8,128)} fusion(f32[16,512,256]{2,1,0:T(8,128)} %reshape.122, f32[512,512]{1,0:T(8,128)} %all-gather.17.cloned.1.call-done), kind=kOutput, calls=%fused_computation.14 | convolution fusion | flops 12884901888 | bytes 17825792 | tf_op jit(solution)/shard_map/sji,spir->spjr/dot_general | solution.py:58
  114.9 9.3 %copy.58 = f32[1,16,512,256]{3,2,1,0:T(8,128)} copy(f32[1,16,512,256]{2,3,1,0:T(8,128)} %convolution_bitcast_fusion.1) | data formatting | bytes 16777216 | tf_op jit(solution)/shard_map/sji,spir->spjr/transpose | solution.py:58
  124.2 9.7 %reshape.125 = f32[4,512,1024]{2,1,0:T(8,128)} reshape(f32[1,16,512,256]{3,2,1,0:T(8,128)} %copy.58) | data formatting | bytes 16777216 | tf_op jit(solution)/shard_map/reshape.9
  133.9 18.2 %fusion.16 = f32[4,1024,512]{1,2,0:T(8,128)S(1)} fusion(f32[4,512,1024]{2,1,0:T(8,128)} %reshape.125, f32[512,512]{1,0:T(8,128)} %all-gather.19.cloned.1.call-done), kind=kOutput, calls=%fused_computation.21 | convolution fusion | flops 12884901888 | bytes 17825792 | tf_op jit(solution)/shard_map/sji,spir->spjr/dot_general | solution.py:58
  152.2 4.1 copy.60
  156.2 5.6 all-to-all-start
  179.1 57.4 %all-gather.21.cloned.1.call-done = f32[512,512]{1,0:T(8,128)} async-done(((f32[128,512]{1,0:T(8,128)}), f32[512,512]{1,0:T(8,128)}) %all-gather.21.cloned.1.call-update) | async-done | bytes 1048592 | tf_op jit(solution)/shard_map/all_gather | solution.py:69
  236.5 3.8 reshape.130
  240.2 37.6 %all-gather.13.cloned.1.call-done = f32[512,512]{1,0:T(8,128)} async-done(((f32[128,512]{1,0:T(8,128)}), f32[512,512]{1,0:T(8,128)}) %all-gather.13.cloned.1.call-update) | async-done | bytes 1048592 | tf_op jit(solution)/shard_map/all_gather | solution.py:39
  279.5 115.9 %all-to-all-done = f32[1,4,4,4,32,1024]{5,4,3,1,0,2:T(8,128)} async-done(((f32[1,4,4,4,32,1024]{5,4,3,1,0,2:T(8,128)}), f32[1,4,4,4,32,1024]{5,4,3,1,0,2:T(8,128)}, u32[]{:S(2)}, u32[]{:S(2)}) %all-to-all-start) | async-done | bytes 8388640 | tf_op jit(solution)/shard_map/all_to_all | solution.py:74
  395.4 4.4 copy.61
  399.9 18.9 %fusion.9 = f32[1,16,4,32,1024]{4,3,1,2,0:T(8,128)S(1)} fusion(f32[16,4,32,1024,1]{3,2,0,4,1:T(8,128)S(1)} %bitcast.122, f32[16,32,16,32]{3,2,1,0:T(8,128)S(1)} %copy-done), kind=kOutput, calls=%fused_computation.15 | convolution fusion | flops 12884901888 | bytes 17825792 | tf_op jit(solution)/shard_map/sabcd,scxdr->saxbr/dot_general | solution.py:76
  418.9 4.1 copy.64
  422.9 9.4 %reshape.131 = f32[4096,512]{1,0:T(8,128)} reshape(f32[1,16,4,32,1024]{4,3,2,1,0:T(8,128)} %copy.64) | data formatting | bytes 16777216 | tf_op jit(solution)/shard_map/reshape.27
  432.3 17.7 %fusion.52 = f32[4096,512]{1,0:T(8,128)} fusion(f32[4096,512]{1,0:T(8,128)} %reshape.131, f32[512,512]{1,0:T(8,128)} %all-gather.23.cloned.1.call-done), kind=kOutput, calls=%fused_computation.95 | convolution fusion | flops 12884901888 | bytes 17825792 | tf_op jit(solution)/shard_map/sji,spi->spj/dot_general | solution.py:52
  450.0 9.4 %reshape.134 = f32[4,4,4,128,256]{4,3,2,1,0:T(8,128)} reshape(f32[4096,512]{1,0:T(8,128)} %fusion.52) | data formatting | bytes 16777216 | tf_op jit(solution)/shard_map/reshape.32
  459.3 16.0 %fusion.6 = f32[1,4,4,4,128,256]{5,4,3,1,2,0:T(8,128)S(1)} fusion(f32[4,4,4,128,256]{4,3,2,1,0:T(8,128)} %reshape.134, f32[4,128,4,128,1,1]{3,2,1,0,5,4:T(4,128)S(1)} %bitcast.123), kind=kOutput, calls=%fused_computation.13 | convolution fusion | flops 12884901888 | bytes 17825792 | tf_op jit(solution)/shard_map/sjce,sacxer->sjaxr/dot_general | solution.py:84
  479.1 9.4 %reduce_sum.66 = f32[16,4,32768]{2,0,1:T(8,128)} reshape(f32[1,4,4,4,128,256]{5,4,2,1,3,0:T(8,128)} %copy.68) | data formatting | bytes 16777216 | tf_op jit(solution)/shard_map/reduce_sum | solution.py:89
  488.5 70.5 %reduce-scatter.2.cloned.1.call-done = f32[16,4,4096]{2,0,1:T(8,128)} async-done(((f32[16,4,32768]{2,0,1:T(8,128)}), f32[16,4,4096]{2,0,1:T(8,128)}) %reduce-scatter.2.cloned.1.call-update) | async-done | bytes 1048592 | tf_op jit(solution)/shard_map/reduce_scatter | solution.py:90
  (58 shorter events, 47.8 us)
Async XLA Ops:
  6.5 42.0 %all-gather.15.cloned.1.call-start = ((), (), s32[]{:S(2)}) async-start(), calls=%async_computation.4 | async-start | bytes 1310720 | tf_op jit(solution)/shard_map/all_gather | solution.py:39
  17.7 66.7 %all-gather.17.cloned.1.call-start = ((), (), s32[]{:S(2)}) async-start(), calls=%async_computation.5 | async-start | bytes 1310720 | tf_op jit(solution)/shard_map/all_gather | solution.py:39
  23.3 110.6 %all-gather.19.cloned.1.call-start = ((), (), s32[]{:S(2)}) async-start(), calls=%async_computation.6 | async-start | bytes 1310720 | tf_op jit(solution)/shard_map/all_gather | solution.py:39
  156.2 239.1 %all-to-all-start = ((f32[1,4,4,4,32,1024]{5,4,3,1,0,2:T(8,128)}), f32[1,4,4,4,32,1024]{5,4,3,1,0,2:T(8,128)}, u32[]{:S(2)}, u32[]{:S(2)}) async-start(f32[1,4,4,4,32,1024]{5,4,3,1,0,2:T(8,128)} %copy.60), calls=%async_computation | async-start | bytes 16777216 | tf_op jit(solution)/shard_map/all_to_all | solution.py:74
  161.9 74.6 %all-gather.21.cloned.1.call-start = ((), (), s32[]{:S(2)}) async-start(), calls=%async_computation.7 | async-start | bytes 1310720 | tf_op jit(solution)/shard_map/all_gather | solution.py:69
  167.7 110.2 %all-gather.13.cloned.1.call-start = ((), (), s32[]{:S(2)}) async-start(), calls=%async_computation.3 | async-start | bytes 1310720 | tf_op jit(solution)/shard_map/all_gather | solution.py:39
  173.3 259.0 %all-gather.23.cloned.1.call-start = ((), (), s32[]{:S(2)}) async-start(), calls=%async_computation.8 | async-start | bytes 1310720 | tf_op jit(solution)/shard_map/all_gather | solution.py:39
  179.0 380.0 %reduce-scatter.2.cloned.1.call-start = ((), (), s32[]{:S(2)}) async-start(), calls=%async_computation.2 | async-start | bytes 9437184 | tf_op jit(solution)/shard_map/reduce_scatter | solution.py:90
  395.4 4.6 copy-start
Sparse Core Ops, SparseCore 0:
  17.8 30.7 all-gather.14
  50.1 27.3 all-gather.16
  79.1 27.3 all-gather.18
  167.8 68.6 all-gather.20
  237.9 39.9 all-gather.12
  279.3 100.0 all-gather.22
  488.6 70.3 reduce-scatter.1
where the time goes:
time: 578 us; the launch traced here: 569 us
  waiting for transfers between devices  292 us (51%)
  matrix products  138 us (24%)
  local copies, waits for them, and re-layouts  115 us (20%)
  between operations  13.9 us (2%)
  starting transfers between devices  5.9 us (1%)
    all_to_all x1, waiting for transfers between devices, per_device(): lax.all_to_all(blocks, 'mode', split_axis=2, concat_axis=1, tiled=True)  116 us
    reduce_scatter x1, waiting for transfers between devices, per_device(): return lax.psum_scatter(summed, 'cuts', scatter_dimension=2, tiled=True)  70.5 us
    all_gather x1, waiting for transfers between devices, per_device(): lax.all_gather(build(picked[:, 3], branch_right(3)), 'mode', axis=1, tile...  57.4 us
    another operation x7, local copies, waits for them, and re-layouts  52.6 us
    dot_general x2, matrix products, kernel(): jnp.einsum('sji,spir->spjr', fragment, shaped, precision=HIGHEST_PRECISION)  48.7 us
    all_gather x5, waiting for transfers between devices, fetch(): lax.all_gather(build(picked[:, branch], branch_right(branch)), 'mode', ax...  47.8 us
    dot_general x2, matrix products, kernel(): jnp.einsum('sji,spi->spj', fragment, shaped, precision=HIGHEST_PRECISION)  35.1 us
    dot_general x6, matrix products, build(): jnp.dot(fragment.reshape(count_a * count_b, width), permuted, precision=H...  19.3 us
  transfers between devices with their start and end apart: 8, of which 5 were waited for; matrix products, arithmetic and copies ran while one was open for 29% of the time, Pallas kernels for 0%

commit v1 on v0

--- a/solution.py
+++ b/solution.py
@@ -2,6 +2,7 @@
 import jax.numpy as jnp
 from jax import lax
 from jax.sharding import PartitionSpec as P
+from jax.lax import all_to_all, psum
 
 HIGHEST_PRECISION = lax.Precision.HIGHEST
 
@@ -71,7 +72,9 @@
     blocks = tensor.reshape(
         slices, leading, devices_mode, columns, inner_head, trailing // inner_head
     )
-    received = lax.all_to_all(blocks, "mode", split_axis=2, concat_axis=1, tiled=True)
+    received = jnp.concatenate(
+        all_to_all(jnp.stack(jnp.split(blocks, psum(1, "mode"), axis=2)), "mode", 0, 0), axis=1
+    )
     arranged = received.reshape(slices, head_states, columns, inner_head, received.shape[5])
     result = jnp.einsum("sabcd,scxdr->saxbr", head_blocks, arranged, precision=HIGHEST_PRECISION)
     tensor = result.reshape(slices, -1)

time: 578 us -> 579 us (level)
  no operation moved by 1% of the time
where the time goes in v1:
time: 579 us; the launch traced here: 570 us
  waiting for transfers between devices  292 us (50%)
  matrix products  138 us (24%)
  local copies, waits for them, and re-layouts  113 us (20%)
  between operations  13.9 us (2%)
  other arithmetic  7.64 us (1%)
  starting transfers between devices  5.91 us (1%)
    all_to_all x1, waiting for transfers between devices, per_device(): all_to_all(jnp.stack(jnp.split(blocks, psum(1, 'mode'), axis=2)), 'mode',...  116 us
    reduce_scatter x1, waiting for transfers between devices, per_device(): return lax.psum_scatter(summed, 'cuts', scatter_dimension=2, tiled=True)  70.5 us
    all_gather x1, waiting for transfers between devices, per_device(): lax.all_gather(build(picked[:, 3], branch_right(3)), 'mode', axis=1, tile...  57.4 us
    another operation x7, local copies, waits for them, and re-layouts  52.6 us
    dot_general x2, matrix products, kernel(): jnp.einsum('sji,spir->spjr', fragment, shaped, precision=HIGHEST_PRECISION)  48.8 us
    all_gather x5, waiting for transfers between devices, fetch(): lax.all_gather(build(picked[:, branch], branch_right(branch)), 'mode', ax...  47.8 us
    dot_general x2, matrix products, kernel(): jnp.einsum('sji,spi->spj', fragment, shaped, precision=HIGHEST_PRECISION)  35.2 us
    dot_general x6, matrix products, build(): jnp.dot(fragment.reshape(count_a * count_b, width), permuted, precision=H...  19.3 us
  transfers between devices with their start and end apart: 8, of which 5 were waited for; matrix products, arithmetic and copies ran while one was open for 29% of the time, Pallas kernels for 0%

profile of v1, /device:TPU:0, one launch (start us, length us, event | category | flops | bytes accessed | tf_op | source)
XLA Modules:
  0.0 570.2 jit_solution(503923572784328235)
XLA Ops:
  29.0 9.4 %reshape.119 = f32[4096,512]{1,0:T(8,128)} reshape(f32[1,4,16,32768]{3,2,1,0:T(8,128)} %param.7) | data formatting | bytes 16777216 | tf_op jit(solution)/shard_map/reshape.2
  38.4 10.2 %all-gather.15.cloned.1.call-done = f32[512,512]{1,0:T(8,128)} async-done(((f32[128,512]{1,0:T(8,128)}), f32[512,512]{1,0:T(8,128)}) %all-gather.15.cloned.1.call-update) | async-done | bytes 1048592 | tf_op jit(solution)/shard_map/all_gather | solution.py:40
  48.6 17.5 %convolution_bitcast_fusion = f32[4096,512]{0,1:T(8,128)} fusion(f32[512,512]{1,0:T(8,128)} %all-gather.15.cloned.1.call-done, f32[4096,512]{1,0:T(8,128)} %reshape.119), kind=kOutput, calls=%fused_computation.10 | convolution fusion | flops 12884901888 | bytes 17825792 | tf_op jit(solution)/shard_map/sji,spi->spj/dot_general | solution.py:53
  66.1 9.0 %copy.43 = f32[4096,512]{1,0:T(8,128)} copy(f32[4096,512]{0,1:T(8,128)} %convolution_bitcast_fusion) | data formatting | bytes 16777216 | tf_op jit(solution)/shard_map/sji,spi->spj/dot_general | solution.py:53
  75.1 9.4 %reshape.120 = f32[16,512,256]{2,1,0:T(8,128)} reshape(f32[4096,512]{1,0:T(8,128)} %copy.43) | data formatting | bytes 16777216 | tf_op jit(solution)/shard_map/reshape.6
  84.5 30.5 %convolution_bitcast_fusion.1 = f32[1,16,512,256]{2,3,1,0:T(8,128)} fusion(f32[16,512,256]{2,1,0:T(8,128)} %reshape.120, f32[512,512]{1,0:T(8,128)} %all-gather.17.cloned.1.call-done), kind=kOutput, calls=%fused_computation.15 | convolution fusion | flops 12884901888 | bytes 17825792 | tf_op jit(solution)/shard_map/sji,spir->spjr/dot_general | solution.py:59
  115.0 9.3 %copy.46 = f32[1,16,512,256]{3,2,1,0:T(8,128)} copy(f32[1,16,512,256]{2,3,1,0:T(8,128)} %convolution_bitcast_fusion.1) | data formatting | bytes 16777216 | tf_op jit(solution)/shard_map/sji,spir->spjr/transpose | solution.py:59
  124.3 9.8 %reshape.123 = f32[4,512,1024]{2,1,0:T(8,128)} reshape(f32[1,16,512,256]{3,2,1,0:T(8,128)} %copy.46) | data formatting | bytes 16777216 | tf_op jit(solution)/shard_map/reshape.9
  134.0 18.2 %fusion.16 = f32[4,1024,512]{1,2,0:T(8,128)S(1)} fusion(f32[4,512,1024]{2,1,0:T(8,128)} %reshape.123, f32[512,512]{1,0:T(8,128)} %all-gather.19.cloned.1.call-done), kind=kOutput, calls=%fused_computation.26 | convolution fusion | flops 12884901888 | bytes 17825792 | tf_op jit(solution)/shard_map/sji,spir->spjr/dot_general | solution.py:59
  157.5 5.7 all-to-all-start
  180.3 57.4 %all-gather.21.cloned.1.call-done = f32[512,512]{1,0:T(8,128)} async-done(((f32[128,512]{1,0:T(8,128)}), f32[512,512]{1,0:T(8,128)}) %all-gather.21.cloned.1.call-update) | async-done | bytes 1048592 | tf_op jit(solution)/shard_map/all_gather | solution.py:70
  237.7 3.8 reshape.128
  241.5 37.6 %all-gather.13.cloned.1.call-done = f32[512,512]{1,0:T(8,128)} async-done(((f32[128,512]{1,0:T(8,128)}), f32[512,512]{1,0:T(8,128)}) %all-gather.13.cloned.1.call-update) | async-done | bytes 1048592 | tf_op jit(solution)/shard_map/all_gather | solution.py:40
  280.8 115.9 %all-to-all-done = f32[4,1,4,1,4,32,1024]{6,5,4,2,3,1,0:T(8,128)} async-done(((f32[4,1,4,1,4,32,1024]{6,5,4,2,3,1,0:T(8,128)}), f32[4,1,4,1,4,32,1024]{6,5,4,2,3,1,0:T(8,128)}, u32[]{:S(2)}, u32[]{:S(2)}) %all-to-all-start) | async-done | bytes 8388640 | tf_op jit(solution)/shard_map/all_to_all | solution.py:76
  396.6 4.4 copy.51
  401.2 18.9 %fusion.9 = f32[1,16,4,32,1024]{4,3,1,2,0:T(8,128)S(1)} fusion(f32[16,4,32,1024,1]{3,2,0,4,1:T(8,128)S(1)} %bitcast.133, f32[16,32,16,32]{3,2,1,0:T(8,128)S(1)} %copy-done), kind=kOutput, calls=%fused_computation.16 | convolution fusion | flops 12884901888 | bytes 17825792 | tf_op jit(solution)/shard_map/sabcd,scxdr->saxbr/dot_general | solution.py:79
  420.2 4.1 copy.54
  424.2 9.4 %reshape.129 = f32[4096,512]{1,0:T(8,128)} reshape(f32[1,16,4,32,1024]{4,3,2,1,0:T(8,128)} %copy.54) | data formatting | bytes 16777216 | tf_op jit(solution)/shard_map/reshape.25
  433.6 17.7 %fusion.52 = f32[4096,512]{1,0:T(8,128)} fusion(f32[4096,512]{1,0:T(8,128)} %reshape.129, f32[512,512]{1,0:T(8,128)} %all-gather.23.cloned.1.call-done), kind=kOutput, calls=%fused_computation.100 | convolution fusion | flops 12884901888 | bytes 17825792 | tf_op jit(solution)/shard_map/sji,spi->spj/dot_general | solution.py:53
  451.2 9.4 %reshape.132 = f32[4,4,4,128,256]{4,3,2,1,0:T(8,128)} reshape(f32[4096,512]{1,0:T(8,128)} %fusion.52) | data formatting | bytes 16777216 | tf_op jit(solution)/shard_map/reshape.30
  460.6 16.0 %fusion.6 = f32[1,4,4,4,128,256]{5,4,3,1,2,0:T(8,128)S(1)} fusion(f32[4,4,4,128,256]{4,3,2,1,0:T(8,128)} %reshape.132, f32[4,128,4,128,1,1]{3,2,1,0,5,4:T(4,128)S(1)} %bitcast.134), kind=kOutput, calls=%fused_computation.14 | convolution fusion | flops 12884901888 | bytes 17825792 | tf_op jit(solution)/shard_map/sjce,sacxer->sjaxr/dot_general | solution.py:87
  476.6 3.8 copy.58
  480.3 9.4 %reduce_sum.66 = f32[16,4,32768]{2,0,1:T(8,128)} reshape(f32[1,4,4,4,128,256]{5,4,2,1,3,0:T(8,128)} %copy.58) | data formatting | bytes 16777216 | tf_op jit(solution)/shard_map/reduce_sum | solution.py:92
  489.8 70.5 %reduce-scatter.2.cloned.1.call-done = f32[16,4,4096]{2,0,1:T(8,128)} async-done(((f32[16,4,32768]{2,0,1:T(8,128)}), f32[16,4,4096]{2,0,1:T(8,128)}) %reduce-scatter.2.cloned.1.call-update) | async-done | bytes 1048592 | tf_op jit(solution)/shard_map/reduce_scatter | solution.py:93
  (59 shorter events, 49.3 us)
Async XLA Ops:
  6.5 42.0 %all-gather.15.cloned.1.call-start = ((), (), s32[]{:S(2)}) async-start(), calls=%async_computation.4 | async-start | bytes 1310720 | tf_op jit(solution)/shard_map/all_gather | solution.py:40
  17.7 66.8 %all-gather.17.cloned.1.call-start = ((), (), s32[]{:S(2)}) async-start(), calls=%async_computation.5 | async-start | bytes 1310720 | tf_op jit(solution)/shard_map/all_gather | solution.py:40
  23.4 110.7 %all-gather.19.cloned.1.call-start = ((), (), s32[]{:S(2)}) async-start(), calls=%async_computation.6 | async-start | bytes 1310720 | tf_op jit(solution)/shard_map/all_gather | solution.py:40
  157.5 239.2 %all-to-all-start = ((f32[4,1,4,1,4,32,1024]{6,5,4,2,3,1,0:T(8,128)}), f32[4,1,4,1,4,32,1024]{6,5,4,2,3,1,0:T(8,128)}, u32[]{:S(2)}, u32[]{:S(2)}) async-start(f32[4,1,4,1,4,32,1024]{6,5,4,2,3,1,0:T(8,128)} %pad_maximum_fusion), calls=%async_computation | async-start | bytes 16777216 | tf_op jit(solution)/shard_map/all_to_all | solution.py:76
  163.1 74.6 %all-gather.21.cloned.1.call-start = ((), (), s32[]{:S(2)}) async-start(), calls=%async_computation.7 | async-start | bytes 1310720 | tf_op jit(solution)/shard_map/all_gather | solution.py:70
  169.0 110.2 %all-gather.13.cloned.1.call-start = ((), (), s32[]{:S(2)}) async-start(), calls=%async_computation.3 | async-start | bytes 1310720 | tf_op jit(solution)/shard_map/all_gather | solution.py:40
  174.6 259.0 %all-gather.23.cloned.1.call-start = ((), (), s32[]{:S(2)}) async-start(), calls=%async_computation.8 | async-start | bytes 1310720 | tf_op jit(solution)/shard_map/all_gather | solution.py:40
  180.3 380.0 %reduce-scatter.2.cloned.1.call-start = ((), (), s32[]{:S(2)}) async-start(), calls=%async_computation.2 | async-start | bytes 9437184 | tf_op jit(solution)/shard_map/reduce_scatter | solution.py:93
  396.6 4.6 copy-start
Sparse Core Ops, SparseCore 0:
  17.8 30.7 all-gather.14
  50.1 27.3 all-gather.16
  79.1 27.3 all-gather.18
  169.1 68.6 all-gather.20
  239.1 39.9 all-gather.12
  280.6 100.0 all-gather.22
  489.9 70.3 reduce-scatter.1
